TPU v7x, 256 devices: a whole 4x4x8 slice. The times are simulated.
256 devices in a mesh: dp: 8 (over x, core), band: 32 (over y, z).
Axes of the slice: x: 4, y: 4, z: 8, core: 2. Of those that a mesh axis runs over, the one named last changes fastest.
Arguments:
- features: bfloat16 [65280, 256], P(('dp', 'band')), parts along dimension 0, may hold values from -6 to 6
- corners: int32 [65280, 512], P(('dp', 'band')), parts along dimension 0, may hold values from 0 to 6143, as said below
- bilinear: float32 [65280, 512], P(('dp', 'band')), parts along dimension 0, may hold values from 0.08 to 0.5, as said below
- attention: float32 [65280, 128], P(('dp', 'band')), parts along dimension 0, may hold values from 0 to 1, as said below
- w_value: bfloat16 [256, 256], replicated, may hold values from -0.375 to 0.375
- b_value: float32 [256], replicated, may hold values from -0.6 to 0.6
- w_out: bfloat16 [256, 256], replicated, may hold values from -1.5 to 1.5
- b_out: float32 [256], replicated, may hold values from -3 to 3
- norm1_gain: float32 [256], replicated, may hold values from 0.5 to 1.5
- norm1_bias: float32 [256], replicated, may hold values from -3 to 3
- w_in: bfloat16 [256, 1024], replicated, may hold values from -0.375 to 0.375
- b_in: float32 [1024], replicated, may hold values from -3 to 3
- w_ffout: bfloat16 [1024, 256], replicated, may hold values from -0.1875 to 0.1875
- b_ffout: float32 [256], replicated, may hold values from -3 to 3
- norm2_gain: float32 [256], replicated, may hold values from 0.5 to 1.5
- norm2_bias: float32 [256], replicated, may hold values from -3 to 3
Outputs:
- encoded: bfloat16 [65280, 256], P(('dp', 'band')), parts along dimension 0
There are 8 independent parts, one for each index of `dp`. A program takes and returns all parts, laid end to end along the dimension named above; an argument that names none is the same for every part. Nothing has to cross between parts.
Inputs may be any that keep to these rules, and one draw needn't show every extreme that they name: An entry for level l is a row of a map of 192 * 32 // 4**l tokens laid out in rows of 128 // 2**l; the four corners of a point are k, k + 1, k + 128 // 2**l and k + 128 // 2**l + 1 in that order. `bilinear`: the four corner weights of a point are positive and sum to one. `attention`: for each token and head the 16 weights are positive and sum to one.
All inputs are finite; a program needn't handle non-finite values.
Results may differ from a plain program's by a relative error of at most 0.009.
Values may be sent and summed in bfloat16 or wider, within the bound.
A program may use at most 64 MiB of HBM per device.

v0:
```python
import jax
import jax.numpy as jnp
from jax import lax
from jax.sharding import Mesh
from jax.sharding import PartitionSpec as P

HEADS = 8
LEVELS = 4
POINTS = 4
ROWS_DEV = 192
BAND = ("band_0", "band_1")
DP_BAND = ("dp", "band_0", "band_1")


def joined_along(pieces, dim):
    pieces = jnp.moveaxis(pieces, 0, dim)
    dims = pieces.shape
    return pieces.reshape(*dims[:dim], dims[dim] * dims[dim + 1], *dims[dim + 2 :])


def stacked_from(shard, axes, order):
    pieces = shard[None]
    for k in order:
        pieces = lax.all_gather(pieces, axes[k], axis=0, tiled=True)
    held = [lax.axis_size(axes[k]) for k in reversed(order)]
    pieces = pieces.reshape(*held, *shard.shape)
    turned = sorted(range(len(order)), key=lambda place: order[len(order) - 1 - place])
    return pieces.transpose(*turned, *range(len(order), pieces.ndim)).reshape(-1, *shard.shape)


def gathered_by_axis(shard, axes, order, dim):
    return joined_along(stacked_from(shard, axes, order), dim)


def layer_norm(inputs, gain, shift):
    average = jnp.mean(inputs, axis=-1, keepdims=True)
    centred = inputs - average
    variance = jnp.mean(centred * centred, axis=-1, keepdims=True)
    return centred * lax.rsqrt(variance + 1e-05) * gain + shift


def blend_rows(place_heads, weight_heads, value_block):
    row_count, model_width = value_block.shape
    head_dim = model_width // HEADS
    lane_groups = -(-row_count // 128)
    padding = lane_groups * 128 - row_count
    padded = jnp.pad(value_block, ((0, padding), (0, 0))).reshape(lane_groups, 128, HEADS, head_dim)
    per_head = jnp.transpose(padded, (2, 0, 1, 3))
    group_ids = jnp.arange(lane_groups, dtype=jnp.int32)
    lane_ids = jnp.arange(128, dtype=jnp.int32)

    def one_head(head_args):
        place_one, weight_one, value_one = head_args
        group_index = place_one // 128
        lane_index = place_one % 128
        group_hits = jnp.where(
            group_index[..., None] == group_ids, weight_one[..., None], jnp.zeros((), jnp.bfloat16)
        )
        lane_hits = (lane_index[..., None] == lane_ids).astype(jnp.bfloat16)
        hit_table = jnp.einsum(
            "qsa,qsb->qab", group_hits, lane_hits, preferred_element_type=jnp.float32
        )
        table_major = hit_table.astype(jnp.bfloat16)
        table_minor = (hit_table - table_major.astype(jnp.float32)).astype(jnp.bfloat16)
        result_major = jnp.einsum(
            "qab,abd->qd", table_major, value_one, preferred_element_type=jnp.float32
        )
        result_minor = jnp.einsum(
            "qab,abd->qd", table_minor, value_one, preferred_element_type=jnp.float32
        )
        return result_major + result_minor

    blended = lax.map(one_head, (place_heads, weight_heads, per_head))
    return jnp.transpose(blended, (1, 0, 2))


def body(
    features,
    corners,
    bilinear,
    attention,
    w_value,
    b_value,
    w_out,
    b_out,
    norm1_gain,
    norm1_bias,
    w_in,
    b_in,
    w_ffout,
    b_ffout,
    norm2_gain,
    norm2_bias,
):
    band_rows, model_width = features.shape
    samples = LEVELS * POINTS * 4
    segment_rows = [ROWS_DEV // 4**level_index for level_index in range(LEVELS)]
    segment_start = [sum(segment_rows[:level_index]) for level_index in range(LEVELS)]
    value_rows = (jnp.dot(features, w_value, preferred_element_type=jnp.float32) + b_value).astype(
        jnp.bfloat16
    )
    weight = (
        attention.reshape(band_rows, HEADS, LEVELS, POINTS, 1)
        * bilinear.reshape(band_rows, HEADS, LEVELS, POINTS, 4)
    ).astype(jnp.bfloat16)
    weight_heads = jnp.transpose(weight.reshape(band_rows, HEADS, samples), (1, 0, 2))
    corner_table = corners.reshape(band_rows, HEADS, LEVELS, POINTS * 4)
    places = []
    for level_index in range(LEVELS):
        level_corner = corner_table[:, :, level_index]
        places.append(
            level_corner // segment_rows[level_index] * band_rows
            + segment_start[level_index]
            + level_corner % segment_rows[level_index]
        )
    place_table = jnp.stack(places, axis=2).reshape(band_rows, HEADS, samples)
    place_heads = jnp.transpose(place_table, (1, 0, 2))
    whole = gathered_by_axis(value_rows, BAND, (0, 1), 0)
    running_sum = blend_rows(place_heads, weight_heads, whole)
    sampled = running_sum.reshape(band_rows, model_width).astype(jnp.bfloat16)
    attended = jnp.dot(sampled, w_out, preferred_element_type=jnp.float32) + b_out
    middle = layer_norm(features.astype(jnp.float32) + attended, norm1_gain, norm1_bias).astype(
        jnp.bfloat16
    )
    hidden = jnp.maximum(
        jnp.dot(middle, w_in, preferred_element_type=jnp.float32) + b_in, 0.0
    ).astype(jnp.bfloat16)
    result = (
        middle.astype(jnp.float32)
        + jnp.dot(hidden, w_ffout, preferred_element_type=jnp.float32)
        + b_ffout
    )
    return layer_norm(result, norm2_gain, norm2_bias).astype(jnp.bfloat16)


def solution(mesh):
    split = Mesh(mesh.devices.reshape(mesh.shape["dp"], 4, 8), ("dp", "band_0", "band_1"))
    return jax.shard_map(
        body,
        mesh=split,
        in_specs=(
            P(DP_BAND, None),
            P(DP_BAND, None),
            P(DP_BAND, None),
            P(DP_BAND, None),
            P(),
            P(),
            P(),
            P(),
            P(),
            P(),
            P(),
            P(),
            P(),
            P(),
            P(),
            P(),
        ),
        out_specs=P(DP_BAND, None),
        check_vma=False,
    )
```

profile of v0, /device:TPU:1, one launch (start us, length us, event | category | flops | bytes accessed | tf_op | source)
XLA Modules:
  0.0 196.2 jit_solution(10287885254114032804)
XLA Ops:
  6.5 1.2 fusion.41
  7.8 13.0 %all-gather.1 = bf16[4,255,256]{2,1,0:T(8,128)(2,1)} all-gather(bf16[1,255,256]{2,1,0:T(8,128)(2,1)S(1)} %fusion.41), channel_id=2, replica_groups=mesh['dp'=8,'band_0'=4,'band_1'=8] {'band_0'}, dimensions={0}, use_global_device_ids=true | all-gather | bytes 652800 | tf_op jit(solution)/shard_map/all_gather | solution.py:24
  20.8 1.2 copy.38
  22.0 1.2 copy.41
  23.3 1.0 copy.39
  24.4 0.3 fusion.42
  24.7 0.5 fusion.46
  25.3 55.0 %all-gather.4.cloned.1.call-done = bf16[32,255,256]{2,1,0:T(8,128)(2,1)} async-done(((bf16[4,255,256]{2,1,0:T(8,128)(2,1)}), bf16[32,255,256]{2,1,0:T(8,128)(2,1)}) %all-gather.4.cloned.1.call-update) | async-done | bytes 4177936 | tf_op jit(solution)/shard_map/all_gather | solution.py:24
  80.3 4.6 %copy.72 = bf16[8,4,255,256]{3,2,0,1:T(8,128)(2,1)} copy(bf16[8,4,255,256]{3,2,1,0:T(8,128)(2,1)} %bitcast.96) | data formatting | bytes 8355840 | tf_op jit(solution)/shard_map/reshape | solution.py:26
  84.9 5.2 %reshape_reshape.3 = bf16[8160,256]{1,0:T(8,128)(2,1)} reshape(bf16[4,8,255,256]{3,2,1,0:T(8,128)(2,1)} %bitcast.94) | data formatting | bytes 8355840 | tf_op jit(solution)/shard_map/reshape;reshape | solution.py:18
  90.1 6.4 %copy.51 = bf16[8160,256]{0,1:T(8,128)(2,1)} copy(bf16[8160,256]{1,0:T(8,128)(2,1)} %reshape_reshape.3) | data formatting | bytes 8355840
  96.5 2.5 %pad_bitcast_fusion = bf16[32,8,64,128]{3,1,2,0:T(8,128)(2,1)S(1)} fusion(bf16[8160,256]{0,1:T(8,128)(2,1)} %copy.51), kind=kLoop, calls=%fused_computation.35 | loop fusion | bytes 8372224
  99.0 3.1 %copy.52 = bf16[32,8,64,128]{3,2,1,0:T(8,128)(2,1)} copy(bf16[32,8,64,128]{3,1,2,0:T(8,128)(2,1)S(1)} %pad_bitcast_fusion) | data formatting | bytes 8388608
  102.2 84.8 %while.13 = (s32[]{:T(128)}, bf16[8,255,32]{1,2,0:T(8,128)(2,1)S(1)}, s32[8,255,64]{1,2,0:T(8,128)S(1)}, bf16[8,255,64]{1,0,2:T(8,128)(2,1)S(1)}, bf16[8,64,128,32]{2,1,3,0:T(8,128)(2,1)}, /*index=5*/s32[]{:T(128)}) while((s32[]{:T(128)}, bf16[8,255,32]{1,2,0:T(8,128)(2,1)S(1)}, s32[8,255,64]{1,2,0:T(8,128)S(1)}, ...), condition=%wide.region_1.2_spmd.clone, body=%wide.region_0.1_spmd.clone.sunk | while | flops 547625728 | bytes 19657812 | solution.py:73
  102.3 0.1 add_select_fusion.11
  102.5 0.1 copy.84
  102.7 3.9 %subtract_convert_fusion.2 = (bf16[255,64,128]{2,1,0:T(8,128)(2,1)S(1)}, bf16[255,64,128]{2,1,0:T(8,128)(2,1)S(1)}) fusion(s32[255,64]{1,0:T(8,128)S(1)} %get-tuple-element.178, s32[255,64]{1,0:T(8,128)S(1)} %get-tuple-element.179, bf16[255,64]{1,0:T(8,128)(2,1)S(1)} %bitcast.99), kind=kOutput, calls=%fused_computation.4.clone.1 | convolution fusion | flops 279920640 | bytes 8519040 | tf_op jit(solution)/shard_map/while/body/eval_jaxpr/qsa,qsb->qab/dot_general | solution.py:60
  106.6 1.1 constant_dynamic-slice_fusion.8
  107.7 2.5 %fusion.83 = f32[255,32]{0,1:T(8,128)S(1)} fusion(bf16[255,64,128]{2,1,0:T(8,128)(2,1)S(1)} %get-tuple-element.180, bf16[1,64,128,32]{2,1,3,0:T(8,128)(2,1)S(1)} %constant_dynamic-slice_fusion.8), kind=kOutput, calls=%fused_computation.15.clone.1 | convolution fusion | flops 133693440 | bytes 4734848 | tf_op jit(solution)/shard_map/while/body/eval_jaxpr/qab,abd->qd/dot_general | solution.py:65
  110.3 2.5 %fusion.84 = bf16[8,255,32]{1,2,0:T(8,128)(2,1)S(1)} fusion(bf16[8,255,32]{1,2,0:T(8,128)(2,1)S(1)} %get-tuple-element.189, s32[]{:T(128)} %get-tuple-element.188, f32[255,32]{0,1:T(8,128)S(1)} %fusion.83, bf16[255,64,128]{2,1,0:T(8,128)(2,1)S(1)} %get-tuple-element.181, bf16[1,64,128,32]{2,1,3,0:T(8,128)(2,1)S(1)} %constant_dynamic-slice_fusion.8), kind=kOutput, calls=%fused_computation.19.clone.1 | convolution fusion | flops 133701600 | bytes 4767748 | tf_op jit(solution)/shard_map/while/body/eval_jaxpr/qab,abd->qd/dot_general | solution.py:68
  112.9 0.1 add_select_fusion.11
  113.1 0.1 copy.84
  113.3 4.0 %subtract_convert_fusion.2 = (bf16[255,64,128]{2,1,0:T(8,128)(2,1)S(1)}, bf16[255,64,128]{2,1,0:T(8,128)(2,1)S(1)}) fusion(s32[255,64]{1,0:T(8,128)S(1)} %get-tuple-element.178, s32[255,64]{1,0:T(8,128)S(1)} %get-tuple-element.179, bf16[255,64]{1,0:T(8,128)(2,1)S(1)} %bitcast.99), kind=kOutput, calls=%fused_computation.4.clone.1 | convolution fusion | flops 279920640 | bytes 8519040 | tf_op jit(solution)/shard_map/while/body/eval_jaxpr/qsa,qsb->qab/dot_general | solution.py:60
  117.2 1.1 constant_dynamic-slice_fusion.8
  118.3 2.5 %fusion.83 = f32[255,32]{0,1:T(8,128)S(1)} fusion(bf16[255,64,128]{2,1,0:T(8,128)(2,1)S(1)} %get-tuple-element.180, bf16[1,64,128,32]{2,1,3,0:T(8,128)(2,1)S(1)} %constant_dynamic-slice_fusion.8), kind=kOutput, calls=%fused_computation.15.clone.1 | convolution fusion | flops 133693440 | bytes 4734848 | tf_op jit(solution)/shard_map/while/body/eval_jaxpr/qab,abd->qd/dot_general | solution.py:65
  120.9 2.5 %fusion.84 = bf16[8,255,32]{1,2,0:T(8,128)(2,1)S(1)} fusion(bf16[8,255,32]{1,2,0:T(8,128)(2,1)S(1)} %get-tuple-element.189, s32[]{:T(128)} %get-tuple-element.188, f32[255,32]{0,1:T(8,128)S(1)} %fusion.83, bf16[255,64,128]{2,1,0:T(8,128)(2,1)S(1)} %get-tuple-element.181, bf16[1,64,128,32]{2,1,3,0:T(8,128)(2,1)S(1)} %constant_dynamic-slice_fusion.8), kind=kOutput, calls=%fused_computation.19.clone.1 | convolution fusion | flops 133701600 | bytes 4767748 | tf_op jit(solution)/shard_map/while/body/eval_jaxpr/qab,abd->qd/dot_general | solution.py:68
  123.5 0.1 add_select_fusion.11
  123.7 0.1 copy.84
  123.9 3.9 %subtract_convert_fusion.2 = (bf16[255,64,128]{2,1,0:T(8,128)(2,1)S(1)}, bf16[255,64,128]{2,1,0:T(8,128)(2,1)S(1)}) fusion(s32[255,64]{1,0:T(8,128)S(1)} %get-tuple-element.178, s32[255,64]{1,0:T(8,128)S(1)} %get-tuple-element.179, bf16[255,64]{1,0:T(8,128)(2,1)S(1)} %bitcast.99), kind=kOutput, calls=%fused_computation.4.clone.1 | convolution fusion | flops 279920640 | bytes 8519040 | tf_op jit(solution)/shard_map/while/body/eval_jaxpr/qsa,qsb->qab/dot_general | solution.py:60
  127.8 1.1 constant_dynamic-slice_fusion.8
  128.9 2.5 %fusion.83 = f32[255,32]{0,1:T(8,128)S(1)} fusion(bf16[255,64,128]{2,1,0:T(8,128)(2,1)S(1)} %get-tuple-element.180, bf16[1,64,128,32]{2,1,3,0:T(8,128)(2,1)S(1)} %constant_dynamic-slice_fusion.8), kind=kOutput, calls=%fused_computation.15.clone.1 | convolution fusion | flops 133693440 | bytes 4734848 | tf_op jit(solution)/shard_map/while/body/eval_jaxpr/qab,abd->qd/dot_general | solution.py:65
  131.5 2.5 %fusion.84 = bf16[8,255,32]{1,2,0:T(8,128)(2,1)S(1)} fusion(bf16[8,255,32]{1,2,0:T(8,128)(2,1)S(1)} %get-tuple-element.189, s32[]{:T(128)} %get-tuple-element.188, f32[255,32]{0,1:T(8,128)S(1)} %fusion.83, bf16[255,64,128]{2,1,0:T(8,128)(2,1)S(1)} %get-tuple-element.181, bf16[1,64,128,32]{2,1,3,0:T(8,128)(2,1)S(1)} %constant_dynamic-slice_fusion.8), kind=kOutput, calls=%fused_computation.19.clone.1 | convolution fusion | flops 133701600 | bytes 4767748 | tf_op jit(solution)/shard_map/while/body/eval_jaxpr/qab,abd->qd/dot_general | solution.py:68
  134.1 0.1 add_select_fusion.11
  134.3 0.1 copy.84
  134.5 4.0 %subtract_convert_fusion.2 = (bf16[255,64,128]{2,1,0:T(8,128)(2,1)S(1)}, bf16[255,64,128]{2,1,0:T(8,128)(2,1)S(1)}) fusion(s32[255,64]{1,0:T(8,128)S(1)} %get-tuple-element.178, s32[255,64]{1,0:T(8,128)S(1)} %get-tuple-element.179, bf16[255,64]{1,0:T(8,128)(2,1)S(1)} %bitcast.99), kind=kOutput, calls=%fused_computation.4.clone.1 | convolution fusion | flops 279920640 | bytes 8519040 | tf_op jit(solution)/shard_map/while/body/eval_jaxpr/qsa,qsb->qab/dot_general | solution.py:60
  138.4 1.1 constant_dynamic-slice_fusion.8
  139.5 2.5 %fusion.83 = f32[255,32]{0,1:T(8,128)S(1)} fusion(bf16[255,64,128]{2,1,0:T(8,128)(2,1)S(1)} %get-tuple-element.180, bf16[1,64,128,32]{2,1,3,0:T(8,128)(2,1)S(1)} %constant_dynamic-slice_fusion.8), kind=kOutput, calls=%fused_computation.15.clone.1 | convolution fusion | flops 133693440 | bytes 4734848 | tf_op jit(solution)/shard_map/while/body/eval_jaxpr/qab,abd->qd/dot_general | solution.py:65
  142.1 2.5 %fusion.84 = bf16[8,255,32]{1,2,0:T(8,128)(2,1)S(1)} fusion(bf16[8,255,32]{1,2,0:T(8,128)(2,1)S(1)} %get-tuple-element.189, s32[]{:T(128)} %get-tuple-element.188, f32[255,32]{0,1:T(8,128)S(1)} %fusion.83, bf16[255,64,128]{2,1,0:T(8,128)(2,1)S(1)} %get-tuple-element.181, bf16[1,64,128,32]{2,1,3,0:T(8,128)(2,1)S(1)} %constant_dynamic-slice_fusion.8), kind=kOutput, calls=%fused_computation.19.clone.1 | convolution fusion | flops 133701600 | bytes 4767748 | tf_op jit(solution)/shard_map/while/body/eval_jaxpr/qab,abd->qd/dot_general | solution.py:68
  144.7 0.1 add_select_fusion.11
  145.0 0.1 copy.84
  145.1 4.0 %subtract_convert_fusion.2 = (bf16[255,64,128]{2,1,0:T(8,128)(2,1)S(1)}, bf16[255,64,128]{2,1,0:T(8,128)(2,1)S(1)}) fusion(s32[255,64]{1,0:T(8,128)S(1)} %get-tuple-element.178, s32[255,64]{1,0:T(8,128)S(1)} %get-tuple-element.179, bf16[255,64]{1,0:T(8,128)(2,1)S(1)} %bitcast.99), kind=kOutput, calls=%fused_computation.4.clone.1 | convolution fusion | flops 279920640 | bytes 8519040 | tf_op jit(solution)/shard_map/while/body/eval_jaxpr/qsa,qsb->qab/dot_general | solution.py:60
  149.0 1.1 constant_dynamic-slice_fusion.8
  150.1 2.5 %fusion.83 = f32[255,32]{0,1:T(8,128)S(1)} fusion(bf16[255,64,128]{2,1,0:T(8,128)(2,1)S(1)} %get-tuple-element.180, bf16[1,64,128,32]{2,1,3,0:T(8,128)(2,1)S(1)} %constant_dynamic-slice_fusion.8), kind=kOutput, calls=%fused_computation.15.clone.1 | convolution fusion | flops 133693440 | bytes 4734848 | tf_op jit(solution)/shard_map/while/body/eval_jaxpr/qab,abd->qd/dot_general | solution.py:65
  152.7 2.5 %fusion.84 = bf16[8,255,32]{1,2,0:T(8,128)(2,1)S(1)} fusion(bf16[8,255,32]{1,2,0:T(8,128)(2,1)S(1)} %get-tuple-element.189, s32[]{:T(128)} %get-tuple-element.188, f32[255,32]{0,1:T(8,128)S(1)} %fusion.83, bf16[255,64,128]{2,1,0:T(8,128)(2,1)S(1)} %get-tuple-element.181, bf16[1,64,128,32]{2,1,3,0:T(8,128)(2,1)S(1)} %constant_dynamic-slice_fusion.8), kind=kOutput, calls=%fused_computation.19.clone.1 | convolution fusion | flops 133701600 | bytes 4767748 | tf_op jit(solution)/shard_map/while/body/eval_jaxpr/qab,abd->qd/dot_general | solution.py:68
  155.6 0.1 copy.84
  155.7 4.0 %subtract_convert_fusion.2 = (bf16[255,64,128]{2,1,0:T(8,128)(2,1)S(1)}, bf16[255,64,128]{2,1,0:T(8,128)(2,1)S(1)}) fusion(s32[255,64]{1,0:T(8,128)S(1)} %get-tuple-element.178, s32[255,64]{1,0:T(8,128)S(1)} %get-tuple-element.179, bf16[255,64]{1,0:T(8,128)(2,1)S(1)} %bitcast.99), kind=kOutput, calls=%fused_computation.4.clone.1 | convolution fusion | flops 279920640 | bytes 8519040 | tf_op jit(solution)/shard_map/while/body/eval_jaxpr/qsa,qsb->qab/dot_general | solution.py:60
  159.6 1.1 constant_dynamic-slice_fusion.8
  160.7 2.5 %fusion.83 = f32[255,32]{0,1:T(8,128)S(1)} fusion(bf16[255,64,128]{2,1,0:T(8,128)(2,1)S(1)} %get-tuple-element.180, bf16[1,64,128,32]{2,1,3,0:T(8,128)(2,1)S(1)} %constant_dynamic-slice_fusion.8), kind=kOutput, calls=%fused_computation.15.clone.1 | convolution fusion | flops 133693440 | bytes 4734848 | tf_op jit(solution)/shard_map/while/body/eval_jaxpr/qab,abd->qd/dot_general | solution.py:65
  163.3 2.5 %fusion.84 = bf16[8,255,32]{1,2,0:T(8,128)(2,1)S(1)} fusion(bf16[8,255,32]{1,2,0:T(8,128)(2,1)S(1)} %get-tuple-element.189, s32[]{:T(128)} %get-tuple-element.188, f32[255,32]{0,1:T(8,128)S(1)} %fusion.83, bf16[255,64,128]{2,1,0:T(8,128)(2,1)S(1)} %get-tuple-element.181, bf16[1,64,128,32]{2,1,3,0:T(8,128)(2,1)S(1)} %constant_dynamic-slice_fusion.8), kind=kOutput, calls=%fused_computation.19.clone.1 | convolution fusion | flops 133701600 | bytes 4767748 | tf_op jit(solution)/shard_map/while/body/eval_jaxpr/qab,abd->qd/dot_general | solution.py:68
  166.2 0.1 copy.84
  166.3 3.9 %subtract_convert_fusion.2 = (bf16[255,64,128]{2,1,0:T(8,128)(2,1)S(1)}, bf16[255,64,128]{2,1,0:T(8,128)(2,1)S(1)}) fusion(s32[255,64]{1,0:T(8,128)S(1)} %get-tuple-element.178, s32[255,64]{1,0:T(8,128)S(1)} %get-tuple-element.179, bf16[255,64]{1,0:T(8,128)(2,1)S(1)} %bitcast.99), kind=kOutput, calls=%fused_computation.4.clone.1 | convolution fusion | flops 279920640 | bytes 8519040 | tf_op jit(solution)/shard_map/while/body/eval_jaxpr/qsa,qsb->qab/dot_general | solution.py:60
  170.3 1.1 constant_dynamic-slice_fusion.8
  171.3 2.5 %fusion.83 = f32[255,32]{0,1:T(8,128)S(1)} fusion(bf16[255,64,128]{2,1,0:T(8,128)(2,1)S(1)} %get-tuple-element.180, bf16[1,64,128,32]{2,1,3,0:T(8,128)(2,1)S(1)} %constant_dynamic-slice_fusion.8), kind=kOutput, calls=%fused_computation.15.clone.1 | convolution fusion | flops 133693440 | bytes 4734848 | tf_op jit(solution)/shard_map/while/body/eval_jaxpr/qab,abd->qd/dot_general | solution.py:65
  173.9 2.5 %fusion.84 = bf16[8,255,32]{1,2,0:T(8,128)(2,1)S(1)} fusion(bf16[8,255,32]{1,2,0:T(8,128)(2,1)S(1)} %get-tuple-element.189, s32[]{:T(128)} %get-tuple-element.188, f32[255,32]{0,1:T(8,128)S(1)} %fusion.83, bf16[255,64,128]{2,1,0:T(8,128)(2,1)S(1)} %get-tuple-element.181, bf16[1,64,128,32]{2,1,3,0:T(8,128)(2,1)S(1)} %constant_dynamic-slice_fusion.8), kind=kOutput, calls=%fused_computation.19.clone.1 | convolution fusion | flops 133701600 | bytes 4767748 | tf_op jit(solution)/shard_map/while/body/eval_jaxpr/qab,abd->qd/dot_general | solution.py:68
  176.8 0.1 copy.84
  176.9 4.0 %subtract_convert_fusion.2 = (bf16[255,64,128]{2,1,0:T(8,128)(2,1)S(1)}, bf16[255,64,128]{2,1,0:T(8,128)(2,1)S(1)}) fusion(s32[255,64]{1,0:T(8,128)S(1)} %get-tuple-element.178, s32[255,64]{1,0:T(8,128)S(1)} %get-tuple-element.179, bf16[255,64]{1,0:T(8,128)(2,1)S(1)} %bitcast.99), kind=kOutput, calls=%fused_computation.4.clone.1 | convolution fusion | flops 279920640 | bytes 8519040 | tf_op jit(solution)/shard_map/while/body/eval_jaxpr/qsa,qsb->qab/dot_general | solution.py:60
  180.9 1.1 constant_dynamic-slice_fusion.8
  181.9 2.5 %fusion.83 = f32[255,32]{0,1:T(8,128)S(1)} fusion(bf16[255,64,128]{2,1,0:T(8,128)(2,1)S(1)} %get-tuple-element.180, bf16[1,64,128,32]{2,1,3,0:T(8,128)(2,1)S(1)} %constant_dynamic-slice_fusion.8), kind=kOutput, calls=%fused_computation.15.clone.1 | convolution fusion | flops 133693440 | bytes 4734848 | tf_op jit(solution)/shard_map/while/body/eval_jaxpr/qab,abd->qd/dot_general | solution.py:65
  184.5 2.5 %fusion.84 = bf16[8,255,32]{1,2,0:T(8,128)(2,1)S(1)} fusion(bf16[8,255,32]{1,2,0:T(8,128)(2,1)S(1)} %get-tuple-element.189, s32[]{:T(128)} %get-tuple-element.188, f32[255,32]{0,1:T(8,128)S(1)} %fusion.83, bf16[255,64,128]{2,1,0:T(8,128)(2,1)S(1)} %get-tuple-element.181, bf16[1,64,128,32]{2,1,3,0:T(8,128)(2,1)S(1)} %constant_dynamic-slice_fusion.8), kind=kOutput, calls=%fused_computation.19.clone.1 | convolution fusion | flops 133701600 | bytes 4767748 | tf_op jit(solution)/shard_map/while/body/eval_jaxpr/qab,abd->qd/dot_general | solution.py:68
  187.1 0.3 fusion.69
  187.4 0.2 multiply_reduce_fusion.1
  187.6 0.7 fusion.70
  188.3 0.2 multiply_reduce_fusion
  188.5 0.8 add_convert_fusion
  (59 shorter events, 2.0 us)
Async XLA Ops:
  6.5 181.1 %copy-start = (bf16[1024,256]{1,0:T(8,128)(2,1)S(1)}, bf16[1024,256]{1,0:T(8,128)(2,1)}, u32[]{:S(2)}) copy-start(bf16[1024,256]{1,0:T(8,128)(2,1)} %param.30) | copy-start | bytes 1572868
  6.5 73.8 %all-gather.4.cloned.1.call-start = ((), (), s32[]{:S(2)}) async-start(), calls=%async_computation | async-start | bytes 4718592 | tf_op jit(solution)/shard_map/all_gather | solution.py:24
  102.1 84.9 %copy-start.1 = (bf16[255,256]{1,0:T(8,128)(2,1)S(1)}, bf16[255,256]{1,0:T(8,128)(2,1)}, u32[]{:S(2)}) copy-start(bf16[255,256]{1,0:T(8,128)(2,1)} %param.18) | copy-start | bytes 391684
  102.1 84.9 %copy-start.2 = (bf16[256,256]{1,0:T(8,128)(2,1)S(1)}, bf16[256,256]{1,0:T(8,128)(2,1)}, u32[]{:S(2)}) copy-start(bf16[256,256]{1,0:T(8,128)(2,1)} %param.24) | copy-start | bytes 393220
  102.1 84.9 %copy-start.3 = (f32[256]{0:T(256)S(1)}, f32[256]{0:T(256)}, u32[]{:S(2)}) copy-start(f32[256]{0:T(256)} %param.25) | copy-start | bytes 3076
  102.1 85.5 %copy-start.6 = (bf16[256,1024]{1,0:T(8,128)(2,1)S(1)}, bf16[256,1024]{1,0:T(8,128)(2,1)}, u32[]{:S(2)}) copy-start(bf16[256,1024]{1,0:T(8,128)(2,1)} %param.28) | copy-start | bytes 1572868
  102.1 85.5 %copy-start.7 = (f32[1024]{0:T(1024)S(1)}, f32[1024]{0:T(1024)}, u32[]{:S(2)}) copy-start(f32[1024]{0:T(1024)} %param.29) | copy-start | bytes 12292
  102.1 85.5 %copy-start.8 = (f32[256]{0:T(256)S(1)}, f32[256]{0:T(256)}, u32[]{:S(2)}) copy-start(f32[256]{0:T(256)} %param.31) | copy-start | bytes 3076
  102.2 85.5 %copy-start.9 = (f32[256]{0:T(256)S(1)}, f32[256]{0:T(256)}, u32[]{:S(2)}) copy-start(f32[256]{0:T(256)} %param.27) | copy-start | bytes 3076
  102.2 85.5 %copy-start.10 = (f32[256]{0:T(256)S(1)}, f32[256]{0:T(256)}, u32[]{:S(2)}) copy-start(f32[256]{0:T(256)} %param.26) | copy-start | bytes 3076
  102.2 86.3 %copy-start.4 = (f32[256]{0:T(256)S(1)}, f32[256]{0:T(256)}, u32[]{:S(2)}) copy-start(f32[256]{0:T(256)} %param.33) | copy-start | bytes 3076
  102.2 86.3 %copy-start.5 = (f32[256]{0:T(256)S(1)}, f32[256]{0:T(256)}, u32[]{:S(2)}) copy-start(f32[256]{0:T(256)} %param.32) | copy-start | bytes 3076
Sparse Core Ops, SparseCore 0:
  20.9 59.3 all-gather.3
where the time goes:
time: 197 us; the launch traced here: 196 us
  matrix products  74.4 us (38%)
  waiting for transfers between devices  55 us (28%)
  local copies, waits for them, and re-layouts  36.6 us (19%)
  between operations  13.6 us (7%)
  blocking collectives  13 us (7%)
  other arithmetic  3.03 us (2%)
    all_gather x1, waiting for transfers between devices, stacked_from(): pieces = lax.all_gather(pieces, axes[k], axis=0, tiled=True)  55 us
    dot_general x8, matrix products, one_head(): jnp.einsum('qsa,qsb->qab', group_hits, lane_hits, preferred_element_type=...  31.6 us
    dot_general x8, matrix products, one_head(): jnp.einsum('qab,abd->qd', table_minor, value_one, preferred_element_type=...  20.3 us
    dot_general x8, matrix products, one_head(): jnp.einsum('qab,abd->qd', table_major, value_one, preferred_element_type=...  20.3 us
    unnamed x28, local copies, waits for them, and re-layouts  15.5 us
    all_gather x1, blocking collectives, stacked_from(): pieces = lax.all_gather(pieces, axes[k], axis=0, tiled=True)  13 us
    dynamic_slice x40, local copies, waits for them, and re-layouts, blend_rows(): blended = lax.map(one_head, (place_heads, weight_heads, per_head))  11.1 us
    another operation x1, local copies, waits for them, and re-layouts, joined_along(): pieces.reshape(*dims[:dim], dims[dim] * dims[dim + 1], *dims[dim + 2:])  5.19 us
  transfers between devices with their start and end apart: 1, of which 1 were waited for; matrix products, arithmetic and copies ran while one was open for 2% of the time, Pallas kernels for 0%

commit v1 on v0

--- a/solution.py
+++ b/solution.py
@@ -21,7 +21,9 @@
 def stacked_from(shard, axes, order):
     pieces = shard[None]
     for k in order:
-        pieces = lax.all_gather(pieces, axes[k], axis=0, tiled=True)
+        pieces = jnp.concatenate(
+            lax.all_to_all(jnp.stack([pieces] * lax.axis_size(axes[k])), axes[k], 0, 0), axis=0
+        )
     held = [lax.axis_size(axes[k]) for k in reversed(order)]
     pieces = pieces.reshape(*held, *shard.shape)
     turned = sorted(range(len(order)), key=lambda place: order[len(order) - 1 - place])

time: 197 us -> 235 us (1.19)
  waiting for transfers between devices: 55 us -> 94.9 us
  between operations: 13.6 us -> 0.27 us
  starting transfers between devices: 0.01 us -> 8.31 us
  local copies, waits for them, and re-layouts: 36.6 us -> 39.6 us
    all_to_all x0 -> x1, waiting for transfers between devices: none -> 94.9 us  [stacked_from(): lax.all_to_all(jnp.stack([pieces] * lax.axis_size(axes[k])), axes[k], 0, 0)]
    all_gather x1 -> x0, waiting for transfers between devices: 55 us -> none  [stacked_from(): pieces = lax.all_gather(pieces, axes[k], axis=0, tiled=True)]
    all_to_all x0 -> x1, blocking collectives: none -> 13.4 us  [stacked_from(): lax.all_to_all(jnp.stack([pieces] * lax.axis_size(axes[k])), axes[k], 0, 0)]
    all_gather x1 -> x0, blocking collectives: 13 us -> none  [stacked_from(): pieces = lax.all_gather(pieces, axes[k], axis=0, tiled=True)]
    unnamed x28 -> x35, local copies, waits for them, and re-layouts: 15.5 us -> 24.9 us
    all_to_all x0 -> x1, starting transfers between devices: none -> 8.31 us  [stacked_from(): lax.all_to_all(jnp.stack([pieces] * lax.axis_size(axes[k])), axes[k], 0, 0)]
    reshape x1 -> x0, local copies, waits for them, and re-layouts: 4.61 us -> none  [stacked_from(): pieces = pieces.reshape(*held, *shard.shape)]
    another operation x1 -> x3, local copies, waits for them, and re-layouts: 5.19 us -> 3.46 us  [stacked_from(): jnp.stack([pieces] * lax.axis_size(axes[k]))]
  transfers between devices with their start and end apart: 1 -> 1, of which waited for: 1 -> 1; matrix products, arithmetic and copies ran while one was open for 2% -> 1% of each run, Pallas kernels for 0% -> 0%
where the time goes in v1:
time: 235 us; the launch traced here: 234 us
  waiting for transfers between devices  94.9 us (40%)
  matrix products  74.4 us (32%)
  local copies, waits for them, and re-layouts  39.6 us (17%)
  blocking collectives  13.4 us (6%)
  starting transfers between devices  8.31 us (4%)
  other arithmetic  3.02 us (1%)
    all_to_all x1, waiting for transfers between devices, stacked_from(): lax.all_to_all(jnp.stack([pieces] * lax.axis_size(axes[k])), axes[k], 0, 0)  94.9 us
    dot_general x8, matrix products, one_head(): jnp.einsum('qsa,qsb->qab', group_hits, lane_hits, preferred_element_type=...  31.6 us
    unnamed x35, local copies, waits for them, and re-layouts  24.9 us
    dot_general x8, matrix products, one_head(): jnp.einsum('qab,abd->qd', table_minor, value_one, preferred_element_type=...  20.3 us
    dot_general x8, matrix products, one_head(): jnp.einsum('qab,abd->qd', table_major, value_one, preferred_element_type=...  20.3 us
    all_to_all x1, blocking collectives, stacked_from(): lax.all_to_all(jnp.stack([pieces] * lax.axis_size(axes[k])), axes[k], 0, 0)  13.4 us
    dynamic_slice x40, local copies, waits for them, and re-layouts, blend_rows(): blended = lax.map(one_head, (place_heads, weight_heads, per_head))  11.1 us
    all_to_all x1, starting transfers between devices, stacked_from(): lax.all_to_all(jnp.stack([pieces] * lax.axis_size(axes[k])), axes[k], 0, 0)  8.31 us
  transfers between devices with their start and end apart: 1, of which 1 were waited for; matrix products, arithmetic and copies ran while one was open for 1% of the time, Pallas kernels for 0%

profile of v1, /device:TPU:1, one launch (start us, length us, event | category | flops | bytes accessed | tf_op | source)
XLA Modules:
  0.0 234.5 jit_solution(12295577622277977156)
XLA Ops:
  0.0 1.2 fusion.40
  1.3 13.4 %all_to_all.10 = bf16[4,1,255,256]{3,2,1,0:T(8,128)(2,1)S(1)} all-to-all(bf16[4,1,255,256]{3,2,1,0:T(8,128)(2,1)S(1)} %stack.14), channel_id=1, replica_groups=mesh['dp'=8,'band_0'=4,'band_1'=8] {'band_0'}, dimensions={0} | all-to-all | bytes 1044480 | tf_op jit(solution)/shard_map/all_to_all | solution.py:25
  14.7 0.4 copy.42
  15.1 3.0 %stack.15 = bf16[8,4,255,256]{3,1,2,0:T(4,128)(2,1)} broadcast(bf16[4,255,256]{2,0,1:T(4,128)(2,1)S(1)} %copy.42), dimensions={1,2,3} | broadcast | bytes 4700160 | tf_op jit(solution)/shard_map/stack | solution.py:25
  18.1 8.3 %all-to-all-start.1 = ((bf16[8,4,255,256]{3,1,2,0:T(4,128)(2,1)}), bf16[8,4,255,256]{3,1,2,0:T(4,128)(2,1)}, u32[]{:S(2)}, u32[]{:S(2)}) async-start(bf16[8,4,255,256]{3,1,2,0:T(4,128)(2,1)} %stack.15), calls=%async_computation.1 | async-start | bytes 8355840 | tf_op jit(solution)/shard_map/all_to_all | solution.py:25
  26.4 0.2 copy.37
  26.7 0.2 copy.40
  27.1 0.3 fusion.41
  27.4 0.5 fusion.45
  28.0 94.9 %all-to-all-done.1 = bf16[8,4,255,256]{3,1,2,0:T(4,128)(2,1)} async-done(((bf16[8,4,255,256]{3,1,2,0:T(4,128)(2,1)}), bf16[8,4,255,256]{3,1,2,0:T(4,128)(2,1)}, u32[]{:S(2)}, u32[]{:S(2)}) %all-to-all-start.1) | async-done | bytes 4177952 | tf_op jit(solution)/shard_map/all_to_all | solution.py:25
  122.9 9.0 %copy.52 = bf16[4,8,255,256]{2,1,0,3:T(8,128)(2,1)} copy(bf16[4,8,255,256]{3,0,2,1:T(4,128)(2,1)} %bitcast.7) | data formatting | bytes 8355840
  131.9 9.7 %reshape.115 = bf16[8160,256]{0,1:T(8,128)(2,1)} reshape(bf16[4,8,255,256]{2,1,0,3:T(8,128)(2,1)} %copy.52) | data formatting | bytes 8355840
  141.6 2.5 %pad_bitcast_fusion = bf16[32,8,64,128]{3,1,2,0:T(8,128)(2,1)S(1)} fusion(bf16[8160,256]{0,1:T(8,128)(2,1)} %reshape.115), kind=kLoop, calls=%fused_computation.35 | loop fusion | bytes 8372224
  144.1 3.1 %copy.54 = bf16[32,8,64,128]{3,2,1,0:T(8,128)(2,1)} copy(bf16[32,8,64,128]{3,1,2,0:T(8,128)(2,1)S(1)} %pad_bitcast_fusion) | data formatting | bytes 8388608
  147.4 84.8 %while.13 = (s32[]{:T(128)}, bf16[8,255,32]{1,2,0:T(8,128)(2,1)S(1)}, s32[8,255,64]{1,2,0:T(8,128)S(1)}, bf16[8,255,64]{1,0,2:T(8,128)(2,1)S(1)}, bf16[8,64,128,32]{2,1,3,0:T(8,128)(2,1)}, /*index=5*/s32[]{:T(128)}) while((s32[]{:T(128)}, bf16[8,255,32]{1,2,0:T(8,128)(2,1)S(1)}, s32[8,255,64]{1,2,0:T(8,128)S(1)}, ...), condition=%wide.region_1.2_spmd.clone, body=%wide.region_0.1_spmd.clone.sunk | while | flops 547625728 | bytes 19657812 | solution.py:75
  147.5 0.1 add_select_fusion.11
  147.7 0.1 copy.84
  147.8 4.0 %subtract_convert_fusion.2 = (bf16[255,64,128]{2,1,0:T(8,128)(2,1)S(1)}, bf16[255,64,128]{2,1,0:T(8,128)(2,1)S(1)}) fusion(s32[255,64]{1,0:T(8,128)S(1)} %get-tuple-element.178, s32[255,64]{1,0:T(8,128)S(1)} %get-tuple-element.179, bf16[255,64]{1,0:T(8,128)(2,1)S(1)} %bitcast.98), kind=kOutput, calls=%fused_computation.4.clone.1 | convolution fusion | flops 279920640 | bytes 8519040 | tf_op jit(solution)/shard_map/while/body/eval_jaxpr/qsa,qsb->qab/dot_general | solution.py:62
  151.8 1.1 constant_dynamic-slice_fusion.8
  152.9 2.5 %fusion.82 = f32[255,32]{0,1:T(8,128)S(1)} fusion(bf16[255,64,128]{2,1,0:T(8,128)(2,1)S(1)} %get-tuple-element.180, bf16[1,64,128,32]{2,1,3,0:T(8,128)(2,1)S(1)} %constant_dynamic-slice_fusion.8), kind=kOutput, calls=%fused_computation.15.clone.1 | convolution fusion | flops 133693440 | bytes 4734848 | tf_op jit(solution)/shard_map/while/body/eval_jaxpr/qab,abd->qd/dot_general | solution.py:67
  155.4 2.5 %fusion.83 = bf16[8,255,32]{1,2,0:T(8,128)(2,1)S(1)} fusion(bf16[8,255,32]{1,2,0:T(8,128)(2,1)S(1)} %get-tuple-element.189, s32[]{:T(128)} %get-tuple-element.188, f32[255,32]{0,1:T(8,128)S(1)} %fusion.82, bf16[255,64,128]{2,1,0:T(8,128)(2,1)S(1)} %get-tuple-element.181, bf16[1,64,128,32]{2,1,3,0:T(8,128)(2,1)S(1)} %constant_dynamic-slice_fusion.8), kind=kOutput, calls=%fused_computation.19.clone.1 | convolution fusion | flops 133701600 | bytes 4767748 | tf_op jit(solution)/shard_map/while/body/eval_jaxpr/qab,abd->qd/dot_general | solution.py:70
  158.1 0.1 add_select_fusion.11
  158.3 0.1 copy.84
  158.4 4.0 %subtract_convert_fusion.2 = (bf16[255,64,128]{2,1,0:T(8,128)(2,1)S(1)}, bf16[255,64,128]{2,1,0:T(8,128)(2,1)S(1)}) fusion(s32[255,64]{1,0:T(8,128)S(1)} %get-tuple-element.178, s32[255,64]{1,0:T(8,128)S(1)} %get-tuple-element.179, bf16[255,64]{1,0:T(8,128)(2,1)S(1)} %bitcast.98), kind=kOutput, calls=%fused_computation.4.clone.1 | convolution fusion | flops 279920640 | bytes 8519040 | tf_op jit(solution)/shard_map/while/body/eval_jaxpr/qsa,qsb->qab/dot_general | solution.py:62
  162.4 1.1 constant_dynamic-slice_fusion.8
  163.5 2.5 %fusion.82 = f32[255,32]{0,1:T(8,128)S(1)} fusion(bf16[255,64,128]{2,1,0:T(8,128)(2,1)S(1)} %get-tuple-element.180, bf16[1,64,128,32]{2,1,3,0:T(8,128)(2,1)S(1)} %constant_dynamic-slice_fusion.8), kind=kOutput, calls=%fused_computation.15.clone.1 | convolution fusion | flops 133693440 | bytes 4734848 | tf_op jit(solution)/shard_map/while/body/eval_jaxpr/qab,abd->qd/dot_general | solution.py:67
  166.0 2.5 %fusion.83 = bf16[8,255,32]{1,2,0:T(8,128)(2,1)S(1)} fusion(bf16[8,255,32]{1,2,0:T(8,128)(2,1)S(1)} %get-tuple-element.189, s32[]{:T(128)} %get-tuple-element.188, f32[255,32]{0,1:T(8,128)S(1)} %fusion.82, bf16[255,64,128]{2,1,0:T(8,128)(2,1)S(1)} %get-tuple-element.181, bf16[1,64,128,32]{2,1,3,0:T(8,128)(2,1)S(1)} %constant_dynamic-slice_fusion.8), kind=kOutput, calls=%fused_computation.19.clone.1 | convolution fusion | flops 133701600 | bytes 4767748 | tf_op jit(solution)/shard_map/while/body/eval_jaxpr/qab,abd->qd/dot_general | solution.py:70
  168.7 0.1 add_select_fusion.11
  168.9 0.1 copy.84
  169.0 4.0 %subtract_convert_fusion.2 = (bf16[255,64,128]{2,1,0:T(8,128)(2,1)S(1)}, bf16[255,64,128]{2,1,0:T(8,128)(2,1)S(1)}) fusion(s32[255,64]{1,0:T(8,128)S(1)} %get-tuple-element.178, s32[255,64]{1,0:T(8,128)S(1)} %get-tuple-element.179, bf16[255,64]{1,0:T(8,128)(2,1)S(1)} %bitcast.98), kind=kOutput, calls=%fused_computation.4.clone.1 | convolution fusion | flops 279920640 | bytes 8519040 | tf_op jit(solution)/shard_map/while/body/eval_jaxpr/qsa,qsb->qab/dot_general | solution.py:62
  173.0 1.1 constant_dynamic-slice_fusion.8
  174.1 2.5 %fusion.82 = f32[255,32]{0,1:T(8,128)S(1)} fusion(bf16[255,64,128]{2,1,0:T(8,128)(2,1)S(1)} %get-tuple-element.180, bf16[1,64,128,32]{2,1,3,0:T(8,128)(2,1)S(1)} %constant_dynamic-slice_fusion.8), kind=kOutput, calls=%fused_computation.15.clone.1 | convolution fusion | flops 133693440 | bytes 4734848 | tf_op jit(solution)/shard_map/while/body/eval_jaxpr/qab,abd->qd/dot_general | solution.py:67
  176.6 2.5 %fusion.83 = bf16[8,255,32]{1,2,0:T(8,128)(2,1)S(1)} fusion(bf16[8,255,32]{1,2,0:T(8,128)(2,1)S(1)} %get-tuple-element.189, s32[]{:T(128)} %get-tuple-element.188, f32[255,32]{0,1:T(8,128)S(1)} %fusion.82, bf16[255,64,128]{2,1,0:T(8,128)(2,1)S(1)} %get-tuple-element.181, bf16[1,64,128,32]{2,1,3,0:T(8,128)(2,1)S(1)} %constant_dynamic-slice_fusion.8), kind=kOutput, calls=%fused_computation.19.clone.1 | convolution fusion | flops 133701600 | bytes 4767748 | tf_op jit(solution)/shard_map/while/body/eval_jaxpr/qab,abd->qd/dot_general | solution.py:70
  179.3 0.1 add_select_fusion.11
  179.5 0.1 copy.84
  179.6 3.9 %subtract_convert_fusion.2 = (bf16[255,64,128]{2,1,0:T(8,128)(2,1)S(1)}, bf16[255,64,128]{2,1,0:T(8,128)(2,1)S(1)}) fusion(s32[255,64]{1,0:T(8,128)S(1)} %get-tuple-element.178, s32[255,64]{1,0:T(8,128)S(1)} %get-tuple-element.179, bf16[255,64]{1,0:T(8,128)(2,1)S(1)} %bitcast.98), kind=kOutput, calls=%fused_computation.4.clone.1 | convolution fusion | flops 279920640 | bytes 8519040 | tf_op jit(solution)/shard_map/while/body/eval_jaxpr/qsa,qsb->qab/dot_general | solution.py:62
  183.6 1.1 constant_dynamic-slice_fusion.8
  184.7 2.5 %fusion.82 = f32[255,32]{0,1:T(8,128)S(1)} fusion(bf16[255,64,128]{2,1,0:T(8,128)(2,1)S(1)} %get-tuple-element.180, bf16[1,64,128,32]{2,1,3,0:T(8,128)(2,1)S(1)} %constant_dynamic-slice_fusion.8), kind=kOutput, calls=%fused_computation.15.clone.1 | convolution fusion | flops 133693440 | bytes 4734848 | tf_op jit(solution)/shard_map/while/body/eval_jaxpr/qab,abd->qd/dot_general | solution.py:67
  187.2 2.5 %fusion.83 = bf16[8,255,32]{1,2,0:T(8,128)(2,1)S(1)} fusion(bf16[8,255,32]{1,2,0:T(8,128)(2,1)S(1)} %get-tuple-element.189, s32[]{:T(128)} %get-tuple-element.188, f32[255,32]{0,1:T(8,128)S(1)} %fusion.82, bf16[255,64,128]{2,1,0:T(8,128)(2,1)S(1)} %get-tuple-element.181, bf16[1,64,128,32]{2,1,3,0:T(8,128)(2,1)S(1)} %constant_dynamic-slice_fusion.8), kind=kOutput, calls=%fused_computation.19.clone.1 | convolution fusion | flops 133701600 | bytes 4767748 | tf_op jit(solution)/shard_map/while/body/eval_jaxpr/qab,abd->qd/dot_general | solution.py:70
  190.1 0.1 copy.84
  190.2 4.0 %subtract_convert_fusion.2 = (bf16[255,64,128]{2,1,0:T(8,128)(2,1)S(1)}, bf16[255,64,128]{2,1,0:T(8,128)(2,1)S(1)}) fusion(s32[255,64]{1,0:T(8,128)S(1)} %get-tuple-element.178, s32[255,64]{1,0:T(8,128)S(1)} %get-tuple-element.179, bf16[255,64]{1,0:T(8,128)(2,1)S(1)} %bitcast.98), kind=kOutput, calls=%fused_computation.4.clone.1 | convolution fusion | flops 279920640 | bytes 8519040 | tf_op jit(solution)/shard_map/while/body/eval_jaxpr/qsa,qsb->qab/dot_general | solution.py:62
  194.2 1.1 constant_dynamic-slice_fusion.8
  195.3 2.5 %fusion.82 = f32[255,32]{0,1:T(8,128)S(1)} fusion(bf16[255,64,128]{2,1,0:T(8,128)(2,1)S(1)} %get-tuple-element.180, bf16[1,64,128,32]{2,1,3,0:T(8,128)(2,1)S(1)} %constant_dynamic-slice_fusion.8), kind=kOutput, calls=%fused_computation.15.clone.1 | convolution fusion | flops 133693440 | bytes 4734848 | tf_op jit(solution)/shard_map/while/body/eval_jaxpr/qab,abd->qd/dot_general | solution.py:67
  197.8 2.5 %fusion.83 = bf16[8,255,32]{1,2,0:T(8,128)(2,1)S(1)} fusion(bf16[8,255,32]{1,2,0:T(8,128)(2,1)S(1)} %get-tuple-element.189, s32[]{:T(128)} %get-tuple-element.188, f32[255,32]{0,1:T(8,128)S(1)} %fusion.82, bf16[255,64,128]{2,1,0:T(8,128)(2,1)S(1)} %get-tuple-element.181, bf16[1,64,128,32]{2,1,3,0:T(8,128)(2,1)S(1)} %constant_dynamic-slice_fusion.8), kind=kOutput, calls=%fused_computation.19.clone.1 | convolution fusion | flops 133701600 | bytes 4767748 | tf_op jit(solution)/shard_map/while/body/eval_jaxpr/qab,abd->qd/dot_general | solution.py:70
  200.7 0.1 copy.84
  200.9 4.0 %subtract_convert_fusion.2 = (bf16[255,64,128]{2,1,0:T(8,128)(2,1)S(1)}, bf16[255,64,128]{2,1,0:T(8,128)(2,1)S(1)}) fusion(s32[255,64]{1,0:T(8,128)S(1)} %get-tuple-element.178, s32[255,64]{1,0:T(8,128)S(1)} %get-tuple-element.179, bf16[255,64]{1,0:T(8,128)(2,1)S(1)} %bitcast.98), kind=kOutput, calls=%fused_computation.4.clone.1 | convolution fusion | flops 279920640 | bytes 8519040 | tf_op jit(solution)/shard_map/while/body/eval_jaxpr/qsa,qsb->qab/dot_general | solution.py:62
  204.8 1.1 constant_dynamic-slice_fusion.8
  205.9 2.5 %fusion.82 = f32[255,32]{0,1:T(8,128)S(1)} fusion(bf16[255,64,128]{2,1,0:T(8,128)(2,1)S(1)} %get-tuple-element.180, bf16[1,64,128,32]{2,1,3,0:T(8,128)(2,1)S(1)} %constant_dynamic-slice_fusion.8), kind=kOutput, calls=%fused_computation.15.clone.1 | convolution fusion | flops 133693440 | bytes 4734848 | tf_op jit(solution)/shard_map/while/body/eval_jaxpr/qab,abd->qd/dot_general | solution.py:67
  208.4 2.5 %fusion.83 = bf16[8,255,32]{1,2,0:T(8,128)(2,1)S(1)} fusion(bf16[8,255,32]{1,2,0:T(8,128)(2,1)S(1)} %get-tuple-element.189, s32[]{:T(128)} %get-tuple-element.188, f32[255,32]{0,1:T(8,128)S(1)} %fusion.82, bf16[255,64,128]{2,1,0:T(8,128)(2,1)S(1)} %get-tuple-element.181, bf16[1,64,128,32]{2,1,3,0:T(8,128)(2,1)S(1)} %constant_dynamic-slice_fusion.8), kind=kOutput, calls=%fused_computation.19.clone.1 | convolution fusion | flops 133701600 | bytes 4767748 | tf_op jit(solution)/shard_map/while/body/eval_jaxpr/qab,abd->qd/dot_general | solution.py:70
  211.3 0.1 copy.84
  211.5 4.0 %subtract_convert_fusion.2 = (bf16[255,64,128]{2,1,0:T(8,128)(2,1)S(1)}, bf16[255,64,128]{2,1,0:T(8,128)(2,1)S(1)}) fusion(s32[255,64]{1,0:T(8,128)S(1)} %get-tuple-element.178, s32[255,64]{1,0:T(8,128)S(1)} %get-tuple-element.179, bf16[255,64]{1,0:T(8,128)(2,1)S(1)} %bitcast.98), kind=kOutput, calls=%fused_computation.4.clone.1 | convolution fusion | flops 279920640 | bytes 8519040 | tf_op jit(solution)/shard_map/while/body/eval_jaxpr/qsa,qsb->qab/dot_general | solution.py:62
  215.4 1.1 constant_dynamic-slice_fusion.8
  216.5 2.5 %fusion.82 = f32[255,32]{0,1:T(8,128)S(1)} fusion(bf16[255,64,128]{2,1,0:T(8,128)(2,1)S(1)} %get-tuple-element.180, bf16[1,64,128,32]{2,1,3,0:T(8,128)(2,1)S(1)} %constant_dynamic-slice_fusion.8), kind=kOutput, calls=%fused_computation.15.clone.1 | convolution fusion | flops 133693440 | bytes 4734848 | tf_op jit(solution)/shard_map/while/body/eval_jaxpr/qab,abd->qd/dot_general | solution.py:67
  219.0 2.5 %fusion.83 = bf16[8,255,32]{1,2,0:T(8,128)(2,1)S(1)} fusion(bf16[8,255,32]{1,2,0:T(8,128)(2,1)S(1)} %get-tuple-element.189, s32[]{:T(128)} %get-tuple-element.188, f32[255,32]{0,1:T(8,128)S(1)} %fusion.82, bf16[255,64,128]{2,1,0:T(8,128)(2,1)S(1)} %get-tuple-element.181, bf16[1,64,128,32]{2,1,3,0:T(8,128)(2,1)S(1)} %constant_dynamic-slice_fusion.8), kind=kOutput, calls=%fused_computation.19.clone.1 | convolution fusion | flops 133701600 | bytes 4767748 | tf_op jit(solution)/shard_map/while/body/eval_jaxpr/qab,abd->qd/dot_general | solution.py:70
  221.9 0.1 copy.84
  222.1 3.9 %subtract_convert_fusion.2 = (bf16[255,64,128]{2,1,0:T(8,128)(2,1)S(1)}, bf16[255,64,128]{2,1,0:T(8,128)(2,1)S(1)}) fusion(s32[255,64]{1,0:T(8,128)S(1)} %get-tuple-element.178, s32[255,64]{1,0:T(8,128)S(1)} %get-tuple-element.179, bf16[255,64]{1,0:T(8,128)(2,1)S(1)} %bitcast.98), kind=kOutput, calls=%fused_computation.4.clone.1 | convolution fusion | flops 279920640 | bytes 8519040 | tf_op jit(solution)/shard_map/while/body/eval_jaxpr/qsa,qsb->qab/dot_general | solution.py:62
  226.0 1.1 constant_dynamic-slice_fusion.8
  227.1 2.5 %fusion.82 = f32[255,32]{0,1:T(8,128)S(1)} fusion(bf16[255,64,128]{2,1,0:T(8,128)(2,1)S(1)} %get-tuple-element.180, bf16[1,64,128,32]{2,1,3,0:T(8,128)(2,1)S(1)} %constant_dynamic-slice_fusion.8), kind=kOutput, calls=%fused_computation.15.clone.1 | convolution fusion | flops 133693440 | bytes 4734848 | tf_op jit(solution)/shard_map/while/body/eval_jaxpr/qab,abd->qd/dot_general | solution.py:67
  229.6 2.5 %fusion.83 = bf16[8,255,32]{1,2,0:T(8,128)(2,1)S(1)} fusion(bf16[8,255,32]{1,2,0:T(8,128)(2,1)S(1)} %get-tuple-element.189, s32[]{:T(128)} %get-tuple-element.188, f32[255,32]{0,1:T(8,128)S(1)} %fusion.82, bf16[255,64,128]{2,1,0:T(8,128)(2,1)S(1)} %get-tuple-element.181, bf16[1,64,128,32]{2,1,3,0:T(8,128)(2,1)S(1)} %constant_dynamic-slice_fusion.8), kind=kOutput, calls=%fused_computation.19.clone.1 | convolution fusion | flops 133701600 | bytes 4767748 | tf_op jit(solution)/shard_map/while/body/eval_jaxpr/qab,abd->qd/dot_general | solution.py:70
  232.2 0.3 fusion.68
  232.5 0.2 multiply_reduce_fusion.1
  232.8 0.7 fusion.69
  233.5 0.2 multiply_reduce_fusion
  233.7 0.8 add_convert_fusion
  (66 shorter events, 2.3 us)
Async XLA Ops:
  0.0 232.7 %copy-start = (bf16[1024,256]{1,0:T(8,128)(2,1)S(1)}, bf16[1024,256]{1,0:T(8,128)(2,1)}, u32[]{:S(2)}) copy-start(bf16[1024,256]{1,0:T(8,128)(2,1)} %param.30) | copy-start | bytes 1572868
  18.1 8.3 %copy-start.2 = (s32[255,512]{1,0:T(8,128)S(1)}, s32[255,512]{1,0:T(8,128)}, u32[]{:S(2)}) copy-start(s32[255,512]{1,0:T(8,128)} %param.19) | copy-start | bytes 1566724
  18.1 8.5 %copy-start.3 = (f32[255,512]{1,0:T(8,128)S(1)}, f32[255,512]{1,0:T(8,128)}, u32[]{:S(2)}) copy-start(f32[255,512]{1,0:T(8,128)} %param.20) | copy-start | bytes 1566724
  18.1 8.7 %copy-start.5 = (f32[255,128]{1,0:T(8,128)S(1)}, f32[255,128]{1,0:T(8,128)}, u32[]{:S(2)}) copy-start(f32[255,128]{1,0:T(8,128)} %param.21) | copy-start | bytes 391684
  18.1 104.8 %all-to-all-start.1 = ((bf16[8,4,255,256]{3,1,2,0:T(4,128)(2,1)}), bf16[8,4,255,256]{3,1,2,0:T(4,128)(2,1)}, u32[]{:S(2)}, u32[]{:S(2)}) async-start(bf16[8,4,255,256]{3,1,2,0:T(4,128)(2,1)} %stack.15), calls=%async_computation.1 | async-start | bytes 8355840 | tf_op jit(solution)/shard_map/all_to_all | solution.py:25
  147.3 84.9 %copy-start.1 = (bf16[255,256]{1,0:T(8,128)(2,1)S(1)}, bf16[255,256]{1,0:T(8,128)(2,1)}, u32[]{:S(2)}) copy-start(bf16[255,256]{1,0:T(8,128)(2,1)} %param.18) | copy-start | bytes 391684
  147.3 84.9 %copy-start.4 = (bf16[256,256]{1,0:T(8,128)(2,1)S(1)}, bf16[256,256]{1,0:T(8,128)(2,1)}, u32[]{:S(2)}) copy-start(bf16[256,256]{1,0:T(8,128)(2,1)} %param.24) | copy-start | bytes 393220
  147.3 84.9 %copy-start.6 = (f32[256]{0:T(256)S(1)}, f32[256]{0:T(256)}, u32[]{:S(2)}) copy-start(f32[256]{0:T(256)} %param.25) | copy-start | bytes 3076
  147.3 85.5 %copy-start.9 = (bf16[256,1024]{1,0:T(8,128)(2,1)S(1)}, bf16[256,1024]{1,0:T(8,128)(2,1)}, u32[]{:S(2)}) copy-start(bf16[256,1024]{1,0:T(8,128)(2,1)} %param.28) | copy-start | bytes 1572868
  147.3 85.5 %copy-start.10 = (f32[1024]{0:T(1024)S(1)}, f32[1024]{0:T(1024)}, u32[]{:S(2)}) copy-start(f32[1024]{0:T(1024)} %param.29) | copy-start | bytes 12292
  147.3 85.5 %copy-start.11 = (f32[256]{0:T(256)S(1)}, f32[256]{0:T(256)}, u32[]{:S(2)}) copy-start(f32[256]{0:T(256)} %param.31) | copy-start | bytes 3076
  147.3 85.5 %copy-start.12 = (f32[256]{0:T(256)S(1)}, f32[256]{0:T(256)}, u32[]{:S(2)}) copy-start(f32[256]{0:T(256)} %param.27) | copy-start | bytes 3076
  147.3 85.5 %copy-start.13 = (f32[256]{0:T(256)S(1)}, f32[256]{0:T(256)}, u32[]{:S(2)}) copy-start(f32[256]{0:T(256)} %param.26) | copy-start | bytes 3076
  147.3 86.3 %copy-start.7 = (f32[256]{0:T(256)S(1)}, f32[256]{0:T(256)}, u32[]{:S(2)}) copy-start(f32[256]{0:T(256)} %param.33) | copy-start | bytes 3076
  147.4 86.3 %copy-start.8 = (f32[256]{0:T(256)S(1)}, f32[256]{0:T(256)}, u32[]{:S(2)}) copy-start(f32[256]{0:T(256)} %param.32) | copy-start | bytes 3076
